TPU v7x, 32 devices: a whole 2x2x4 slice. The times are simulated.
32 devices in a mesh: section: 4 (over y, x), owner: 8 (over z, core).
Axes of the slice: x: 2, y: 2, z: 4, core: 2. Of those that a mesh axis runs over, the one named last changes fastest.
Arguments:
- probe_values: bfloat16 [8, 8192, 128], P('section', 'owner'), may hold values from -6 to 6
- probe_keys: int32 [8, 8192], P('section', 'owner'), may hold values from 0 to 2047
- group_ids: int32 [8, 8192], P('section', 'owner'), may hold values from 0 to 127
- block_dest: int32 [8, 64, 1], P('section', 'owner'), may hold values from 0 to 7; in each aligned block of 8 rows (0 to 7, 8 to 15, ..., all dimensions but the last counted through in order) at most 2 rows name the same one
- filter_bits: int32 [4, 8, 512], P('section', None, 'owner'), may hold values from 0 to 65535, as said below
- section_weights: bfloat16 [4, 128, 128], P('section'), may hold values from -0.5 to 0.5
- build_keys: int32 [32768], P('owner'), may hold values from 0 to 2047
- build_values: bfloat16 [32768, 128], P('owner'), may hold values from -6 to 6
Outputs:
- group_sums: float32 [128, 128], P(('section', 'owner'))
Inputs may be any that keep to these rules, and one draw needn't show every extreme that they name: `block_dest`: in each micro-batch, no owner is named by more than 2 of the 8 blocks of one device, a bound that some block reaches. `filter_bits`: bit b of a word is the keep bit of row 16 w + b; the upper bits are 0.
All inputs are finite; a program needn't handle non-finite values.
Results may differ from a plain program's by a relative error of at most 0.012.
Values may be sent and summed in bfloat16 or wider, within the bound.
No kernel may reach another device: no remote copies, remote signals or barrier semaphores. Data moves between devices by JAX's collectives and lax.ppermute only.
A program may use at most 128 MiB of HBM per device.

v0:
```python
import jax
import jax.numpy as jnp
from jax import lax
from jax.sharding import PartitionSpec as P

CAP = 2
KEYS_OWN = 2048
GRP_DEV = 4


def unpack_bits(bit_words):
    shifts = jnp.arange(16, dtype=jnp.int32)
    spread = jnp.right_shift(bit_words[..., None], shifts) & 1
    return spread.reshape(bit_words.shape[:-1] + (bit_words.shape[-1] * 16,)).astype(jnp.float32)


def apply_section(payload, kept_mask, weight):
    columns = payload.shape[-1]
    projected = jnp.dot(payload.reshape(-1, columns), weight, preferred_element_type=jnp.float32)
    projected = projected.reshape(payload.shape)
    updated = kept_mask[..., None] * (payload.astype(jnp.float32) + jax.nn.silu(projected))
    return updated.astype(jnp.bfloat16)


def pick_blocks(table_rows, picks):
    return jnp.take(table_rows, picks.reshape(-1), axis=0).reshape(
        picks.shape + table_rows.shape[1:]
    )


def local(
    probe_values,
    probe_keys,
    group_ids,
    block_dest,
    filter_bits,
    section_weights,
    build_keys,
    build_values,
):
    section_count = lax.axis_size("section")
    owner_count = lax.axis_size("owner")
    section_index = lax.axis_index("section")
    batches = probe_values.shape[0]
    block_count = block_dest.shape[1]
    columns = probe_values.shape[2]
    block_rows = probe_values.shape[1] // block_count
    groups_all = GRP_DEV * section_count * owner_count
    payload = probe_values
    all_weights, all_bits = (
        lax.all_gather(section_weights, "section", axis=0, tiled=True),
        lax.all_gather(filter_bits, "section", axis=0, tiled=True),
    )
    for step_number in range(section_count):
        source_section = (section_index + step_number) % section_count
        weight = lax.dynamic_index_in_dim(all_weights, source_section, 0, keepdims=False)
        section_bits = lax.dynamic_index_in_dim(all_bits, source_section, 0, keepdims=False)
        bit_words = lax.dynamic_slice_in_dim(section_bits, section_index * batches, batches, 0)
        payload = apply_section(payload, unpack_bits(bit_words), weight)
    row_keys, row_groups, row_dest = (probe_keys, group_ids, block_dest)
    destination = row_dest[:, :, 0]
    owner_ids = jnp.arange(owner_count, dtype=jnp.int32)
    chosen = (destination[:, :, None] == owner_ids).astype(jnp.int32)
    earlier = jnp.cumsum(chosen, axis=1) - chosen
    slot_index = jnp.sum(earlier * chosen, axis=2)
    capacity = CAP
    slot_ids = jnp.arange(capacity, dtype=jnp.int32)
    matching = chosen[:, :, :, None] * (slot_index[:, :, None, None] == slot_ids).astype(jnp.int32)
    block_ids = jnp.arange(block_count, dtype=jnp.int32)
    source_block = (
        jnp.sum(matching * (block_ids[None, :, None, None] - block_count), axis=1) + block_count
    )
    blocks = payload.reshape(batches, block_count, block_rows, columns)
    blocks = jnp.concatenate(
        [blocks, jnp.zeros((batches, 1, block_rows, columns), jnp.bfloat16)], axis=1
    )
    key_blocks = row_keys.reshape(batches, block_count, block_rows)
    key_blocks = jnp.concatenate(
        [key_blocks, jnp.zeros((batches, 1, block_rows), jnp.int32)], axis=1
    )
    group_blocks = row_groups.reshape(batches, block_count, block_rows)
    group_blocks = jnp.concatenate(
        [group_blocks, jnp.zeros((batches, 1, block_rows), jnp.int32)], axis=1
    )
    send_values = jax.vmap(pick_blocks)(blocks, source_block)
    send_keys = jax.vmap(pick_blocks)(key_blocks, source_block)
    send_groups = jax.vmap(pick_blocks)(group_blocks, source_block)
    key_table = jax.ops.segment_sum(
        build_values.astype(jnp.float32), build_keys, num_segments=KEYS_OWN
    )
    group_range = jnp.arange(groups_all, dtype=jnp.int32)
    group_span = min(owner_count, 8)

    def add_block(running, pieces):
        part_values, part_keys, part_groups = pieces
        matched = jnp.take(key_table, part_keys, axis=0)
        joined = (part_values.astype(jnp.float32) * matched).astype(jnp.bfloat16)
        onehot = (part_groups[:, None] == group_range).astype(jnp.bfloat16)
        running = running + lax.dot_general(
            onehot, joined, (((0,), (0,)), ((), ())), preferred_element_type=jnp.float32
        )
        return (running, None)

    def join_item(received_item):
        item_values, item_keys, item_groups = received_item
        sources = item_values.shape[0]
        steps_count = sources // group_span
        rows_values = item_values.reshape(steps_count, -1, columns)
        rows_keys = item_keys.reshape(steps_count, -1)
        rows_groups = item_groups.reshape(steps_count, -1)
        running, unused = lax.scan(
            add_block,
            jnp.zeros((groups_all, columns), jnp.float32),
            (rows_values, rows_keys, rows_groups),
        )
        return running

    partials = lax.map(
        join_item,
        (
            lax.all_to_all(send_values, "owner", split_axis=1, concat_axis=1, tiled=True),
            lax.all_to_all(send_keys, "owner", split_axis=1, concat_axis=1, tiled=True),
            lax.all_to_all(send_groups, "owner", split_axis=1, concat_axis=1, tiled=True),
        ),
    )
    partial_sum = jnp.sum(partials, axis=0)
    return lax.psum_scatter(partial_sum, ("section", "owner"), scatter_dimension=0, tiled=True)


def solution(mesh):
    placed = (
        P("section", "owner", None),
        P("section", "owner"),
        P("section", "owner"),
        P("section", "owner", None),
        P("section", None, "owner"),
        P("section", None, None),
        P("owner"),
        P("owner", None),
    )
    return jax.shard_map(
        local, mesh=mesh, in_specs=placed, out_specs=P(("section", "owner"), None), check_vma=False
    )
```

profile of v0, /device:TPU:0, one launch (start us, length us, event | category | flops | bytes accessed | tf_op | source)
XLA Modules:
  0.0 221.8 jit_solution(11686983459232994365)
XLA Ops:
  6.5 0.8 fusion.20
  7.4 0.9 select_reduce_fusion
  8.7 0.7 concatenate.11
  9.4 0.7 concatenate.9
  10.1 0.7 gather_fusion.3
  10.7 0.7 gather_fusion.2
  12.1 6.4 %all-to-all-start = ((s32[2,8,2,128]{3,2,0,1:T(2,128)}), s32[2,8,2,128]{3,2,0,1:T(2,128)S(1)}, u32[]{:S(2)}, u32[]{:S(2)}) async-start(s32[2,8,2,128]{3,2,0,1:T(2,128)} %copy.28), calls=%async_computation | async-start | bytes 32768 | tf_op jit(solution)/shard_map/all_to_all | solution.py:123
  18.5 8.7 %all_gather.7 = bf16[4,128,128]{2,1,0:T(8,128)(2,1)S(1)} all-gather(bf16[1,128,128]{2,1,0:T(8,128)(2,1)} %param.17), channel_id=1, replica_groups=mesh['section'=4,'owner'=8] {'section'}, dimensions={0}, use_global_device_ids=true | all-gather | bytes 163840 | tf_op jit(solution)/shard_map/all_gather | solution.py:51
  28.2 7.9 %all_gather.6 = s32[4,8,64]{2,1,0:T(8,128)S(1)} all-gather(s32[1,8,64]{2,1,0:T(8,128)S(1)} %copy-done.2), channel_id=1, replica_groups=mesh['section'=4,'owner'=8] {'section'}, dimensions={0}, use_global_device_ids=true | all-gather | bytes 10240 | tf_op jit(solution)/shard_map/all_gather | solution.py:52
  37.2 1.6 multiply_convert_fusion.2
  40.7 0.8 gather_fusion.1
  41.5 5.1 %all-to-all-start.2 = ((s32[2,8,2,128]{3,2,0,1:T(2,128)}), s32[2,8,2,128]{3,2,0,1:T(2,128)S(1)}, u32[]{:S(2)}, u32[]{:S(2)}) async-start(s32[2,8,2,128]{3,2,0,1:T(2,128)} %copy.35), calls=%async_computation.2 | async-start | bytes 32768 | tf_op jit(solution)/shard_map/all_to_all | solution.py:122
  46.8 1.1 copy.34
  47.9 4.4 %all-to-all-done.2 = s32[2,8,2,128]{3,2,0,1:T(2,128)S(1)} async-done(((s32[2,8,2,128]{3,2,0,1:T(2,128)}), s32[2,8,2,128]{3,2,0,1:T(2,128)S(1)}, u32[]{:S(2)}, u32[]{:S(2)}) %all-to-all-start.2) | async-done | bytes 16416 | tf_op jit(solution)/shard_map/all_to_all | solution.py:122
  52.2 3.6 %all-to-all-start.1 = ((bf16[2,8,2,128,128]{4,3,2,0,1:T(8,128)(2,1)}), bf16[2,8,2,128,128]{4,3,2,0,1:T(8,128)(2,1)S(1)}, u32[]{:S(2)}, u32[]{:S(2)}) async-start(bf16[2,8,2,128,128]{4,3,2,0,1:T(8,128)(2,1)} %copy.34), calls=%async_computation.1 | async-start | bytes 2097152 | tf_op jit(solution)/shard_map/all_to_all | solution.py:121
  55.9 22.8 %scatter_custom_fusion = f32[2048,128]{1,0:T(8,128)S(1)} fusion(s32[4096]{0:T(1024)} %param.18, bf16[4096,128]{1,0:T(8,128)(2,1)S(1)} %copy-done, f32[]{:T(128)} %constant.200.clone.1), kind=kCustom, calls=%fused_computation.23 | custom fusion | flops 1048576 | bytes 2097664 | tf_op jit(solution)/shard_map/scatter-add | solution.py:88
  78.7 3.6 %all-to-all-done.1 = bf16[2,8,2,128,128]{4,3,2,0,1:T(8,128)(2,1)S(1)} async-done(((bf16[2,8,2,128,128]{4,3,2,0,1:T(8,128)(2,1)}), bf16[2,8,2,128,128]{4,3,2,0,1:T(8,128)(2,1)S(1)}, u32[]{:S(2)}, u32[]{:S(2)}) %all-to-all-start.1) | async-done | bytes 1048608 | tf_op jit(solution)/shard_map/all_to_all | solution.py:121
  82.3 13.3 %while.11 = (s32[]{:T(128)}, f32[2,128,128]{2,1,0:T(8,128)S(1)}, s32[2,8,2,128]{3,2,0,1:T(2,128)S(1)}, bf16[2,8,2,128,128]{4,3,2,0,1:T(8,128)(2,1)S(1)}, s32[2,8...) while((s32[]{:T(128)}, f32[2,128,128]{2,1,0:T(8,128)S(1)}, ...), condition=%wide.region_5.7_spmd.clone, body=%wide.region_4.6_spmd.clone.sunk | while | flops 68440064 | bytes 4878425 | solution.py:118
  82.3 5.5 %gather_fusion = f32[2048,128]{1,0:T(8,128)S(1)} fusion(f32[2048,128]{1,0:T(8,128)S(1)} %get-tuple-element.183, s32[2048]{0:T(1024)S(1)} %broadcast_clamp_fusion.2), kind=kCustom, calls=%fused_computation.1.clone.clone.1 | custom fusion | bytes 2105344 | tf_op jit(solution)/shard_map/while/body/eval_jaxpr/while/body/eval_jaxpr/jit(_take)/gather | solution.py:96
  87.9 1.0 fusion.39
  89.0 5.5 %gather_fusion = f32[2048,128]{1,0:T(8,128)S(1)} fusion(f32[2048,128]{1,0:T(8,128)S(1)} %get-tuple-element.183, s32[2048]{0:T(1024)S(1)} %broadcast_clamp_fusion.2), kind=kCustom, calls=%fused_computation.1.clone.clone.1 | custom fusion | bytes 2105344 | tf_op jit(solution)/shard_map/while/body/eval_jaxpr/while/body/eval_jaxpr/jit(_take)/gather | solution.py:96
  94.5 1.0 fusion.39
  96.2 117.4 %all-reduce.6.cloned.1.call-done = f32[128,128]{1,0:T(8,128)} async-done(((f32[128,128]{1,0:T(8,128)}), f32[128,128]{1,0:T(8,128)}) %all-reduce.6.cloned.1.call-update) | async-done | bytes 65552
  213.7 1.3 constant_dynamic-slice_fusion.7
  (59 shorter events, 6.0 us)
Async XLA Ops:
  6.5 20.7 %copy-start.1 = (bf16[2,1024,128]{2,1,0:T(8,128)(2,1)S(1)}, bf16[2,1024,128]{2,1,0:T(8,128)(2,1)}, u32[]{:S(2)}) copy-start(bf16[2,1024,128]{2,1,0:T(8,128)(2,1)} %param.12) | copy-start | bytes 1572868
  12.1 29.4 %all-to-all-start = ((s32[2,8,2,128]{3,2,0,1:T(2,128)}), s32[2,8,2,128]{3,2,0,1:T(2,128)S(1)}, u32[]{:S(2)}, u32[]{:S(2)}) async-start(s32[2,8,2,128]{3,2,0,1:T(2,128)} %copy.28), calls=%async_computation | async-start | bytes 32768 | tf_op jit(solution)/shard_map/all_to_all | solution.py:123
  27.5 0.7 copy-start.2
  41.5 10.8 %all-to-all-start.2 = ((s32[2,8,2,128]{3,2,0,1:T(2,128)}), s32[2,8,2,128]{3,2,0,1:T(2,128)S(1)}, u32[]{:S(2)}, u32[]{:S(2)}) async-start(s32[2,8,2,128]{3,2,0,1:T(2,128)} %copy.35), calls=%async_computation.2 | async-start | bytes 32768 | tf_op jit(solution)/shard_map/all_to_all | solution.py:122
  47.9 8.0 %copy-start = (bf16[4096,128]{1,0:T(8,128)(2,1)S(1)}, bf16[4096,128]{1,0:T(8,128)(2,1)}, u32[]{:S(2)}) copy-start(bf16[4096,128]{1,0:T(8,128)(2,1)} %param.19) | copy-start | bytes 3145732
  52.2 30.1 %all-to-all-start.1 = ((bf16[2,8,2,128,128]{4,3,2,0,1:T(8,128)(2,1)}), bf16[2,8,2,128,128]{4,3,2,0,1:T(8,128)(2,1)S(1)}, u32[]{:S(2)}, u32[]{:S(2)}) async-start(bf16[2,8,2,128,128]{4,3,2,0,1:T(8,128)(2,1)} %copy.34), calls=%async_computation.1 | async-start | bytes 2097152 | tf_op jit(solution)/shard_map/all_to_all | solution.py:121
  55.8 157.9 %all-reduce.6.cloned.1.call-start = ((), (), s32[]{:S(2)}) async-start(), calls=%async_computation.3 | async-start | bytes 131072
Sparse Core Ops, SparseCore 0:
  96.3 117.2 all-reduce.5
where the time goes:
time: 224 us; the launch traced here: 222 us
  waiting for transfers between devices  125 us (56%)
  other arithmetic  25.6 us (11%)
  local copies, waits for them, and re-layouts  20.3 us (9%)
  blocking collectives  16.6 us (7%)
  starting transfers between devices  15.1 us (7%)
  between operations  13.6 us (6%)
  matrix products  5.02 us (2%)
    unnamed x2, waiting for transfers between devices  117 us
    scatter-add x1, other arithmetic, local(): jax.ops.segment_sum(build_values.astype(jnp.float32), build_keys, num_seg...  22.8 us
    gather x2, local copies, waits for them, and re-layouts, add_block(): matched = jnp.take(key_table, part_keys, axis=0)  10.9 us
    all_gather x1, blocking collectives, local(): lax.all_gather(section_weights, 'section', axis=0, tiled=True)  8.67 us
    all_gather x1, blocking collectives, local(): lax.all_gather(filter_bits, 'section', axis=0, tiled=True)  7.95 us
    all_to_all x1, starting transfers between devices, local(): lax.all_to_all(send_groups, 'owner', split_axis=1, concat_axis=1, tiled=T...  6.35 us
    all_to_all x1, starting transfers between devices, local(): lax.all_to_all(send_keys, 'owner', split_axis=1, concat_axis=1, tiled=True)  5.11 us
  transfers between devices with their start and end apart: 4, of which 3 were waited for; matrix products, arithmetic and copies ran while one was open for 14% of the time, Pallas kernels for 0%

commit v1 on v0

v1 whole, which is shorter than its diff:
```python
import functools

import jax
import jax.numpy as jnp
from jax import lax
from jax.experimental import pallas as pl
from jax.experimental.pallas import tpu as pltpu
from jax.sharding import PartitionSpec as P

CAP = 2
KEYS_OWN = 2048
GRP_DEV = 4
META = 16
BF16 = jnp.bfloat16
F32 = jnp.float32


def vmem():
    return pl.BlockSpec(memory_space=pltpu.VMEM)


def smem():
    return pl.BlockSpec(memory_space=pltpu.SMEM)


def params():
    return pltpu.CompilerParams(vmem_limit_bytes=56 * 2**20)


def walk_blocks(dest_ref, count_ref, owners, batches, blocks, visit):
    def clear(owner, carry):
        count_ref[owner] = 0
        return carry

    lax.fori_loop(0, owners, clear, 0)
    for micro in range(batches):

        def step(block, carry, micro=micro):
            owner = dest_ref[micro, block]
            slot = count_ref[owner]
            count_ref[owner] = slot + 1
            visit(micro, block, owner, slot)
            return carry

        lax.fori_loop(0, blocks, step, 0, unroll=min(blocks, 8))


def pack_first(early, rows, dest_ref, values_ref, keys_ref, groups_ref, out_ref, meta_ref, count_ref):
    owners = out_ref.shape[0]
    batches, blocks = dest_ref.shape
    meta_ref[...] = jnp.zeros_like(meta_ref)
    out_ref[...] = jnp.zeros_like(out_ref)

    def visit(micro, block, owner, slot):
        lanes = pl.ds(pl.multiple_of(block * rows, rows), rows)

        @pl.when(slot < early)
        def _():
            out_ref[owner, pl.ds(pl.multiple_of(slot * rows, rows), rows), :] = values_ref[micro * blocks + block]
            keys = keys_ref[pl.ds(micro, 1), lanes]
            groups = groups_ref[pl.ds(micro, 1), lanes]
            base = slot * 4
            meta_ref[owner, pl.ds(base, 1), :] = (keys >> 7).astype(F32)
            meta_ref[owner, pl.ds(base + 1, 1), :] = (keys & 127).astype(F32)
            meta_ref[owner, pl.ds(base + 2, 1), :] = (groups >> 7).astype(F32)
            meta_ref[owner, pl.ds(base + 3, 1), :] = (groups & 127).astype(F32)

    walk_blocks(dest_ref, count_ref, owners, batches, blocks, visit)
    out_ref[:, early * rows :, :] = meta_ref[...].astype(BF16)


def pack_last(early, rows, dest_ref, values_ref, keys_ref, groups_ref, bits_ref, out_ref, meta_ref, kept_ref, count_ref):
    owners = out_ref.shape[0]
    batches, blocks = dest_ref.shape
    late_slots = (out_ref.shape[1] - META) // rows
    meta_ref[...] = jnp.zeros_like(meta_ref)
    out_ref[...] = jnp.zeros_like(out_ref)
    mask_base = late_slots * 4
    all_kept = bits_ref[0].astype(F32)
    for section in range(1, bits_ref.shape[0]):
        all_kept = all_kept * bits_ref[section].astype(F32)
    kept_ref[...] = all_kept

    def visit(micro, block, owner, slot):
        lanes = pl.ds(pl.multiple_of(block * rows, rows), rows)
        meta_ref[owner, pl.ds(mask_base + slot, 1), :] = kept_ref[pl.ds(micro * blocks + block, 1), :]

        @pl.when(slot >= early)
        def _():
            late = slot - early
            out_ref[owner, pl.ds(pl.multiple_of(late * rows, rows), rows), :] = values_ref[micro * blocks + block]
            keys = keys_ref[pl.ds(micro, 1), lanes]
            groups = groups_ref[pl.ds(micro, 1), lanes]
            base = late * 4
            meta_ref[owner, pl.ds(base, 1), :] = (keys >> 7).astype(F32)
            meta_ref[owner, pl.ds(base + 1, 1), :] = (keys & 127).astype(F32)
            meta_ref[owner, pl.ds(base + 2, 1), :] = (groups >> 7).astype(F32)
            meta_ref[owner, pl.ds(base + 3, 1), :] = (groups & 127).astype(F32)

    walk_blocks(dest_ref, count_ref, owners, batches, blocks, visit)
    out_ref[:, late_slots * rows :, :] = meta_ref[...].astype(BF16)


def build_table(keys_ref, values_ref, out_ref):
    columns = values_ref.shape[1]
    chunks, lanes = keys_ref.shape
    tiles = out_ref.shape[0] // lanes
    sub = lax.broadcasted_iota(jnp.int32, (lanes, lanes), 0)
    low, high = [], []
    for chunk in range(chunks):
        row = keys_ref[pl.ds(chunk, 1), :]
        low.append(jnp.where(sub == (row & (lanes - 1)), 1.0, 0.0).astype(BF16))
        high.append(row >> 7)

    def tile_step(tile, carry):
        hot = [
            low[chunk] * jnp.broadcast_to(jnp.where(high[chunk] == tile, 1.0, 0.0), (lanes, lanes)).astype(BF16)
            for chunk in range(chunks)
        ]
        total = jnp.dot(jnp.concatenate(hot, axis=1), values_ref[...], preferred_element_type=F32)
        head = total.astype(BF16)
        place = pl.ds(pl.multiple_of(tile * lanes, lanes), lanes)
        out_ref[place, :columns] = head
        out_ref[place, columns:] = (total - head.astype(F32)).astype(BF16)
        return carry

    lax.fori_loop(0, tiles, tile_step, 0)


def join_rows(values, meta_columns, table_ref, weights):
    for weight in weights:
        half = jnp.dot(values, weight, preferred_element_type=F32) * 0.5
        values = (values.astype(F32) + (half + half * jnp.tanh(half))).astype(BF16)
    columns = values.shape[1]
    tiles = table_ref.shape[0] // 128
    hot = []
    for high, low in meta_columns:
        rows = high.shape[0]
        lane = lax.broadcasted_iota(jnp.int32, (rows, 128), 1).astype(F32)
        one = jnp.where(lane == low, 1.0, 0.0)
        hot.append(jnp.concatenate([jnp.where(high == float(t), one, 0.0).astype(BF16) for t in range(tiles)], axis=1))
    found = jnp.dot(jnp.concatenate(hot, axis=0), table_ref[...], preferred_element_type=F32)
    matched = found[:, :columns] + found[:, columns:]
    return (values.astype(F32) * matched).astype(BF16)


def pick_weights(weights_ref, home):
    sections = weights_ref.shape[0]
    return [weights_ref[lax.rem(home + j, sections)] for j in range(sections)]


def join_first(early, rows, home_ref, first_ref, weights_ref, table_ref, out_ref):
    weights = pick_weights(weights_ref, home_ref[0])

    def step(source, carry):
        meta = first_ref[source, early * rows :, :].astype(F32)
        turned = meta.T
        pairs = [(turned[:, 4 * j : 4 * j + 1], turned[:, 4 * j + 1 : 4 * j + 2]) for j in range(early)]
        out_ref[source] = join_rows(first_ref[source, : early * rows, :], pairs, table_ref, weights)
        return carry

    lax.fori_loop(0, first_ref.shape[0], step, 0)


def group_hot(groups, high, low, kept):
    group = jnp.where(kept > 0.5, high * 128.0 + low, -1.0)
    sub = lax.broadcasted_iota(jnp.int32, (groups, group.shape[1]), 0).astype(F32)
    return jnp.where(sub == group, 1.0, 0.0).astype(BF16)


def join_last(early, rows, home_ref, first_ref, last_ref, joined_ref, weights_ref, table_ref, out_ref):
    weights = pick_weights(weights_ref, home_ref[0])
    groups = out_ref.shape[0]
    late = (last_ref.shape[1] - META) // rows
    out_ref[...] = jnp.zeros_like(out_ref)

    def step(source, carry):
        early_meta = first_ref[source, early * rows :, :].astype(F32)
        late_meta = last_ref[source, late * rows :, :].astype(F32)
        kept = late_meta[4 * late : 4 * late + early + late]
        turned = late_meta.T
        pairs = [(turned[:, 4 * j : 4 * j + 1], turned[:, 4 * j + 1 : 4 * j + 2]) for j in range(late)]
        fresh = join_rows(last_ref[source, : late * rows, :], pairs, table_ref, weights)
        hot = [
            group_hot(groups, early_meta[4 * j + 2 : 4 * j + 3], early_meta[4 * j + 3 : 4 * j + 4], kept[j : j + 1])
            for j in range(early)
        ] + [
            group_hot(
                groups, late_meta[4 * j + 2 : 4 * j + 3], late_meta[4 * j + 3 : 4 * j + 4], kept[early + j : early + j + 1]
            )
            for j in range(late)
        ]
        joined = jnp.concatenate([joined_ref[source], fresh], axis=0)
        out_ref[...] += jnp.dot(jnp.concatenate(hot, axis=1), joined, preferred_element_type=F32)
        return carry

    lax.fori_loop(0, first_ref.shape[0], step, 0)


def unpack_bits(bit_words):
    shifts = jnp.arange(16, dtype=jnp.int32)
    spread = jnp.right_shift(bit_words[..., None], shifts) & 1
    return spread.reshape(bit_words.shape[:-1] + (bit_words.shape[-1] * 16,))


def local(
    probe_values,
    probe_keys,
    group_ids,
    block_dest,
    filter_bits,
    section_weights,
    build_keys,
    build_values,
):
    sections = lax.axis_size("section")
    owners = lax.axis_size("owner")
    batches, block_count = block_dest.shape[:2]
    columns = probe_values.shape[2]
    rows = probe_values.shape[1] // block_count
    groups_all = GRP_DEV * sections * owners
    slots = batches * CAP
    late = 1
    early = slots - late

    dest = block_dest.reshape(batches, block_count)
    blocks = probe_values.reshape(batches * block_count, rows, columns)
    first = pl.pallas_call(
        functools.partial(pack_first, early, rows),
        out_shape=jax.ShapeDtypeStruct((owners, early * rows + META, columns), BF16),
        in_specs=[smem(), vmem(), vmem(), vmem()],
        out_specs=vmem(),
        scratch_shapes=[pltpu.VMEM((owners, META, columns), F32), pltpu.SMEM((owners,), jnp.int32)],
        compiler_params=params(),
        name="pack_first",
    )(dest, blocks, probe_keys, group_ids)
    first = lax.all_to_all(first, "owner", split_axis=0, concat_axis=0, tiled=True)

    bits = unpack_bits(filter_bits[0]).astype(BF16).reshape(sections, batches * block_count, rows)
    shared = jnp.concatenate([jnp.broadcast_to(section_weights, (sections, columns, columns)), bits], axis=1)
    shared = lax.all_to_all(shared, "section", split_axis=0, concat_axis=0, tiled=True)
    weights = shared[:, :columns]
    bits = shared[:, columns:]

    table = pl.pallas_call(
        build_table,
        out_shape=jax.ShapeDtypeStruct((KEYS_OWN, 2 * columns), BF16),
        in_specs=[vmem(), vmem()],
        out_specs=vmem(),
        compiler_params=params(),
        cost_estimate=pl.CostEstimate(flops=2 * KEYS_OWN * build_keys.shape[0] * columns, bytes_accessed=2**21, transcendentals=0),
        name="build_table",
    )(build_keys.reshape(-1, 128), build_values)

    last = pl.pallas_call(
        functools.partial(pack_last, early, rows),
        out_shape=jax.ShapeDtypeStruct((owners, late * rows + META, columns), BF16),
        in_specs=[smem(), vmem(), vmem(), vmem(), vmem()],
        out_specs=vmem(),
        scratch_shapes=[
            pltpu.VMEM((owners, META, columns), F32),
            pltpu.VMEM((batches * block_count, rows), F32),
            pltpu.SMEM((owners,), jnp.int32),
        ],
        compiler_params=params(),
        name="pack_last",
    )(dest, blocks, probe_keys, group_ids, bits)
    last = lax.all_to_all(last, "owner", split_axis=0, concat_axis=0, tiled=True)

    home = lax.axis_index("section").astype(jnp.int32).reshape(1)
    joined = pl.pallas_call(
        functools.partial(join_first, early, rows),
        out_shape=jax.ShapeDtypeStruct((owners, early * rows, columns), BF16),
        in_specs=[smem(), vmem(), vmem(), vmem()],
        out_specs=vmem(),
        compiler_params=params(),
        cost_estimate=pl.CostEstimate(
            flops=2 * KEYS_OWN * owners * early * rows * 2 * columns, bytes_accessed=2**21, transcendentals=0
        ),
        name="join_first",
    )(home, first, weights, table)
    sums = pl.pallas_call(
        functools.partial(join_last, early, rows),
        out_shape=jax.ShapeDtypeStruct((groups_all, columns), F32),
        in_specs=[smem(), vmem(), vmem(), vmem(), vmem(), vmem()],
        out_specs=vmem(),
        compiler_params=params(),
        cost_estimate=pl.CostEstimate(
            flops=2 * KEYS_OWN * owners * late * rows * 2 * columns, bytes_accessed=2**21, transcendentals=0
        ),
        name="join_last",
    )(home, first, last, joined, weights, table)
    parts = sums.reshape(sections * owners, GRP_DEV, columns)
    parts = lax.all_to_all(parts, ("section", "owner"), split_axis=0, concat_axis=0, tiled=True)
    return jnp.sum(parts, axis=0)


def solution(mesh):
    placed = (
        P("section", "owner", None),
        P("section", "owner"),
        P("section", "owner"),
        P("section", "owner", None),
        P("section", None, "owner"),
        P("section", None, None),
        P("owner"),
        P("owner", None),
    )
    return jax.shard_map(
        local, mesh=mesh, in_specs=placed, out_specs=P(("section", "owner"), None), check_vma=False
    )
```

time: 224 us -> 88.8 us (0.40)
  waiting for transfers between devices: 125 us -> 21.7 us
  Pallas kernels: 0 us -> 36 us
  other arithmetic: 25.6 us -> 1.3 us
  local copies, waits for them, and re-layouts: 20.3 us -> 3.76 us
  between operations: 13.6 us -> 0.06 us
  matrix products: 5.02 us -> 0 us
  blocking collectives: 16.6 us -> 11.9 us
    unnamed x2 -> x0, waiting for transfers between devices: 117 us -> none
    pallas_call x0 -> x5, Pallas kernels: none -> 36 us  [the longest x1 13 us: local(): pl.pallas_call(functools.partial(join_first, early, rows), out_shape=jax....]
    scatter-add x1 -> x0, other arithmetic: 22.8 us -> none  [local(): jax.ops.segment_sum(build_values.astype(jnp.float32), build_keys, num_seg...]
    all_gather x2 -> x0, blocking collectives: 16.6 us -> none  [the longest x1 8.67 us: local(): lax.all_gather(section_weights, 'section', axis=0, tiled=True)]
    all_to_all x3, waiting for transfers between devices: 8.01 us -> 21.7 us  [the longest x1 19 us: local(): lax.all_to_all(first, 'owner', split_axis=0, concat_axis=0, tiled=True)]
    gather x7 -> x0, local copies, waits for them, and re-layouts: 13.2 us -> none  [the longest x2 10.9 us: add_block(): matched = jnp.take(key_table, part_keys, axis=0)]
    all_to_all x0 -> x1, blocking collectives: none -> 11.9 us  [local(): lax.all_to_all(parts, ('section', 'owner'), split_axis=0, concat_axis=0,...]
    dot_general x6 -> x0, matrix products: 5.02 us -> none  [the longest x4 2.95 us: apply_section(): jnp.dot(payload.reshape(-1, columns), weight, preferred_element_type=jnp....]
  transfers between devices with their start and end apart: 4 -> 3, of which waited for: 3 -> 2; matrix products, arithmetic and copies ran while one was open for 14% -> 1% of each run, Pallas kernels for 0% -> 30%
where the time goes in v1:
time: 88.8 us; the launch traced here: 88.2 us
  Pallas kernels  36 us (41%)
  waiting for transfers between devices  21.7 us (24%)
  starting transfers between devices  13.5 us (15%)
  blocking collectives  11.9 us (13%)
  local copies, waits for them, and re-layouts  3.76 us (4%)
  other arithmetic  1.3 us (1%)
    all_to_all x1, waiting for transfers between devices, local(): lax.all_to_all(first, 'owner', split_axis=0, concat_axis=0, tiled=True)  19 us
    pallas_call x1, Pallas kernels, local(): pl.pallas_call(functools.partial(join_first, early, rows), out_shape=jax....  13 us
    all_to_all x1, blocking collectives, local(): lax.all_to_all(parts, ('section', 'owner'), split_axis=0, concat_axis=0,...  11.9 us
    pallas_call x1, Pallas kernels, local(): pl.pallas_call(build_table, out_shape=jax.ShapeDtypeStruct((KEYS_OWN, 2 *...  9.31 us
    pallas_call x1, Pallas kernels, local(): pl.pallas_call(functools.partial(join_last, early, rows), out_shape=jax.S...  9.24 us
    all_to_all x1, starting transfers between devices, local(): lax.all_to_all(shared, 'section', split_axis=0, concat_axis=0, tiled=True)  5.19 us
    all_to_all x1, starting transfers between devices, local(): lax.all_to_all(first, 'owner', split_axis=0, concat_axis=0, tiled=True)  4.88 us
    all_to_all x1, starting transfers between devices, local(): lax.all_to_all(last, 'owner', split_axis=0, concat_axis=0, tiled=True)  3.42 us
  transfers between devices with their start and end apart: 3, of which 2 were waited for; matrix products, arithmetic and copies ran while one was open for 1% of the time, Pallas kernels for 30%

profile of v1, /device:TPU:0, one launch (start us, length us, event | category | flops | bytes accessed | tf_op | source)
XLA Modules:
  0.0 88.2 jit_solution(8529135753193919934)
XLA Ops:
  0.0 0.1 shift_right_arithmetic.31
  0.1 0.7 copy-done.3
  0.8 0.1 shift_right_arithmetic.28
  0.9 0.1 shift_right_arithmetic.29
  1.0 0.0 copy-start.2
  1.1 0.7 copy-done.2
  1.8 0.7 pad_maximum_fusion
  2.5 5.2 %all-to-all-start.1 = ((bf16[4,144,128]{2,1,0:T(8,128)(2,1)}), bf16[4,144,128]{2,1,0:T(8,128)(2,1)S(1)}, u32[]{:S(2)}, u32[]{:S(2)}) async-start(bf16[4,144,128]{2,1,0:T(8,128)(2,1)} %pad_maximum_fusion), calls=%async_computation.1 | async-start | bytes 294912 | tf_op jit(solution)/shard_map/all_to_all | solution.py:241
  7.7 2.3 %pack_first.1 = bf16[8,400,128]{2,1,0:T(8,128)(2,1)} custom-call(s32[2,8]{1,0:T(2,128)} %bitcast.14, bf16[16,128,128]{2,1,0:T(8,128)(2,1)} %bitcast.9, s32[2,1024]{1,0:T(2,128)} %keys_ref.3, s32[2,1024]{1,0:T(2,128)} %groups_ref.3), custom_call_target="tpu_custom_call" | custom-call | tf_op jit(solution)/shard_map/pack_first/pallas_call | solution.py:228
  10.0 2.7 %all-to-all-done.1 = bf16[4,144,128]{2,1,0:T(8,128)(2,1)S(1)} async-done(((bf16[4,144,128]{2,1,0:T(8,128)(2,1)}), bf16[4,144,128]{2,1,0:T(8,128)(2,1)S(1)}, u32[]{:S(2)}, u32[]{:S(2)}) %all-to-all-start.1) | async-done | bytes 147488 | tf_op jit(solution)/shard_map/all_to_all | solution.py:241
  12.8 4.9 %all-to-all-start = ((bf16[8,400,128]{2,1,0:T(8,128)(2,1)}), bf16[8,400,128]{2,1,0:T(8,128)(2,1)S(1)}, u32[]{:S(2)}, u32[]{:S(2)}) async-start(bf16[8,400,128]{2,1,0:T(8,128)(2,1)} %pack_first.1), calls=%async_computation | async-start | bytes 1638400 | tf_op jit(solution)/shard_map/all_to_all | solution.py:237
  17.6 0.6 slice.8.bits_ref
  18.2 2.1 %pack_last.1 = bf16[8,144,128]{2,1,0:T(8,128)(2,1)} custom-call(s32[2,8]{1,0:T(2,128)} %bitcast.15, bf16[16,128,128]{2,1,0:T(8,128)(2,1)} %bitcast.10, s32[2,1024]{1,0:T(2,128)} %keys_ref.3, s32[2,1024]{1,0:T(2,128)} %groups_ref.3, bf16[4,16,128]{2,1,0:T(8,128)(2,1)} %slice.8.bits_ref), custom_call_target="tpu_custom_call" | custom-call | tf_op jit(solution)/shard_map/pack_last/pallas_call | solution.py:255
  20.3 19.0 %all-to-all-done.first_ref = bf16[8,400,128]{2,1,0:T(8,128)(2,1)S(1)} async-done(((bf16[8,400,128]{2,1,0:T(8,128)(2,1)}), bf16[8,400,128]{2,1,0:T(8,128)(2,1)S(1)}, u32[]{:S(2)}, u32[]{:S(2)}) %all-to-all-start) | async-done | bytes 819232 | tf_op jit(solution)/shard_map/all_to_all | solution.py:237
  39.3 3.4 %all-to-all-start.2 = ((bf16[8,144,128]{2,1,0:T(8,128)(2,1)}), bf16[8,144,128]{2,1,0:T(8,128)(2,1)S(1)}, u32[]{:S(2)}, u32[]{:S(2)}) async-start(bf16[8,144,128]{2,1,0:T(8,128)(2,1)} %pack_last.1), calls=%async_computation.2 | async-start | bytes 589824 | tf_op jit(solution)/shard_map/all_to_all | solution.py:268
  42.7 9.3 %build_table.1.table_ref = bf16[2048,256]{1,0:T(8,128)(2,1)} custom-call(s32[32,128]{1,0:T(8,128)} %bitcast.16, bf16[4096,128]{1,0:T(8,128)(2,1)} %values_ref.1), custom_call_target="tpu_custom_call" | custom-call | flops 2147483648 | bytes 2097152 | tf_op jit(solution)/shard_map/build_table/pallas_call | solution.py:245
  52.0 0.0 copy-done
  52.0 0.7 slice.9.weights_ref
  52.7 13.0 %join_first.1.joined_ref = bf16[8,384,128]{2,1,0:T(8,128)(2,1)} custom-call(s32[1]{0:T(128)} %bitcast.home_ref, bf16[8,400,128]{2,1,0:T(8,128)(2,1)} %copy-done, bf16[4,128,128]{2,1,0:T(8,128)(2,1)} %slice.9.weights_ref, bf16[2048,256]{1,0:T(8,128)(2,1)} %build_table.1.table_ref), custom_call_target="tpu_custom_call" | custom-call | flops 3221225472 | bytes 2097152 | tf_op jit(solution)/shard_map/join_first/pallas_call | solution.py:271
  65.7 0.0 all-to-all-done.2.last_ref
  65.7 0.7 copy-done.1
  66.4 9.2 %join_last.1 = f32[128,128]{1,0:T(8,128)} custom-call(s32[1]{0:T(128)} %bitcast.home_ref, bf16[8,400,128]{2,1,0:T(8,128)(2,1)} %copy-done, bf16[8,144,128]{2,1,0:T(8,128)(2,1)} %copy-done.1, bf16[8,384,128]{2,1,0:T(8,128)(2,1)} %join_first.1.joined_ref, bf16[4,128,128]{2,1,0:T(8,128)(2,1)} %slice.9.weights_ref, bf16[2048,256]{1,0:T(8,128)(2,1)} %build_table.1.table_ref), custom_call_target="tpu_custom_call" | custom-call | flops 1073741824 | bytes 2097152 | tf_op jit(solution)/shard_map/join_last/pallas_call | solution.py:282
  75.6 11.9 %all_to_all.20 = f32[32,4,128]{2,1,0:T(4,128)S(1)} all-to-all(f32[32,4,128]{2,1,0:T(4,128)} %bitcast.11), channel_id=1, replica_groups=mesh['section'=4,'owner'=8] {'section','owner'}, dimensions={0} | all-to-all | bytes 131072 | tf_op jit(solution)/shard_map/all_to_all | solution.py:294
  87.5 0.6 reduce_sum.9
  (7 shorter events, 0.0 us)
Async XLA Ops:
  0.1 0.7 copy-start.3
  1.0 0.8 copy-start.2
  2.5 10.3 %all-to-all-start.1 = ((bf16[4,144,128]{2,1,0:T(8,128)(2,1)}), bf16[4,144,128]{2,1,0:T(8,128)(2,1)S(1)}, u32[]{:S(2)}, u32[]{:S(2)}) async-start(bf16[4,144,128]{2,1,0:T(8,128)(2,1)} %pad_maximum_fusion), calls=%async_computation.1 | async-start | bytes 294912 | tf_op jit(solution)/shard_map/all_to_all | solution.py:241
  12.8 26.5 %all-to-all-start = ((bf16[8,400,128]{2,1,0:T(8,128)(2,1)}), bf16[8,400,128]{2,1,0:T(8,128)(2,1)S(1)}, u32[]{:S(2)}, u32[]{:S(2)}) async-start(bf16[8,400,128]{2,1,0:T(8,128)(2,1)} %pack_first.1), calls=%async_computation | async-start | bytes 1638400 | tf_op jit(solution)/shard_map/all_to_all | solution.py:237
  39.3 12.8 %copy-start = (bf16[8,400,128]{2,1,0:T(8,128)(2,1)}, bf16[8,400,128]{2,1,0:T(8,128)(2,1)S(1)}, u32[]{:S(2)}) copy-start(bf16[8,400,128]{2,1,0:T(8,128)(2,1)S(1)} %all-to-all-done.first_ref) | copy-start | bytes 2457604
  39.3 26.4 %all-to-all-start.2 = ((bf16[8,144,128]{2,1,0:T(8,128)(2,1)}), bf16[8,144,128]{2,1,0:T(8,128)(2,1)S(1)}, u32[]{:S(2)}, u32[]{:S(2)}) async-start(bf16[8,144,128]{2,1,0:T(8,128)(2,1)} %pack_last.1), calls=%async_computation.2 | async-start | bytes 589824 | tf_op jit(solution)/shard_map/all_to_all | solution.py:268
  65.7 0.7 copy-start.1

commit v2 on v0

v2 whole, which is shorter than its diff:
```python
import functools
import math

import jax
import jax.numpy as jnp
from jax import lax
from jax.experimental import pallas as pl
from jax.experimental.pallas import tpu as pltpu
from jax.sharding import PartitionSpec as P

CAP = 2
KEYS_OWN = 2048
GRP_DEV = 4
FIELDS = 4
BF16 = jnp.bfloat16
F32 = jnp.float32
I32 = jnp.int32


def run(kernel, name, ins, outs, scratch=(), scalars=0, flops=0):
    several = isinstance(outs, list)
    shapes = [jax.ShapeDtypeStruct(shape, dtype) for shape, dtype in (outs if several else [outs])]
    held = [x for x in ins[scalars:]] + shapes
    size = sum(math.prod(x.shape) * x.dtype.itemsize for x in held)
    for entry in scratch:
        size += 2 * math.prod(getattr(entry, "shape", ())) * 4
    place = pl.BlockSpec(memory_space=pltpu.VMEM)
    return pl.pallas_call(
        kernel,
        out_shape=shapes if several else shapes[0],
        in_specs=[pl.BlockSpec(memory_space=pltpu.SMEM)] * scalars + [place] * (len(ins) - scalars),
        out_specs=[place] * len(shapes) if several else place,
        scratch_shapes=list(scratch),
        compiler_params=pltpu.CompilerParams(vmem_limit_bytes=size + 4 * 2**20),
        cost_estimate=pl.CostEstimate(flops=flops, bytes_accessed=size, transcendentals=0) if flops else None,
        name=name,
    )(*ins)


def walk_blocks(dest_ref, count_ref, owners, visit):
    batches, blocks = dest_ref.shape

    def clear(owner, carry):
        count_ref[owner] = 0
        return carry

    lax.fori_loop(0, owners, clear, 0)
    for micro in range(batches):

        def step(block, carry, micro=micro):
            owner = dest_ref[micro, block]
            slot = count_ref[owner]
            count_ref[owner] = slot + 1
            visit(micro, block, owner, slot)
            return carry

        lax.fori_loop(0, blocks, step, 0, unroll=min(blocks, 8))


def pack_blocks(slots, dest_ref, values_ref, keys_ref, groups_ref, out_ref, meta_ref, count_ref):
    owners = out_ref.shape[0]
    blocks = dest_ref.shape[1]
    rows = values_ref.shape[1]
    meta_ref[...] = jnp.zeros_like(meta_ref)
    out_ref[...] = jnp.zeros_like(out_ref)

    def visit(micro, block, owner, slot):
        lanes = pl.ds(pl.multiple_of(block * rows, rows), rows)
        out_ref[owner, pl.ds(pl.multiple_of(slot * rows, rows), rows), :] = values_ref[micro * blocks + block]
        keys = keys_ref[pl.ds(micro, 1), lanes]
        groups = groups_ref[pl.ds(micro, 1), lanes]
        for field, part in enumerate((keys >> 7, keys & 127, groups >> 7, groups & 127)):
            meta_ref[owner, pl.ds(field * slots + slot, 1), :] = part.astype(F32)

    walk_blocks(dest_ref, count_ref, owners, visit)
    out_ref[:, slots * rows :, :] = meta_ref[...].astype(BF16)


def build_table(keys_ref, values_ref, out_ref):
    chunks, lanes = keys_ref.shape
    tiles = out_ref.shape[0] // lanes
    sub = lax.broadcasted_iota(I32, (lanes, lanes), 0)
    low, high = [], []
    for chunk in range(chunks):
        row = keys_ref[pl.ds(chunk, 1), :]
        low.append(jnp.where(sub == (row & (lanes - 1)), 1.0, 0.0).astype(BF16))
        high.append(row >> 7)

    def tile_step(tile, carry):
        hot = [
            low[chunk] * jnp.broadcast_to(jnp.where(high[chunk] == tile, 1.0, 0.0), (lanes, lanes)).astype(BF16)
            for chunk in range(chunks)
        ]
        place = pl.ds(pl.multiple_of(tile * lanes, lanes), lanes)
        out_ref[place, :] = jnp.dot(jnp.concatenate(hot, axis=1), values_ref[...], preferred_element_type=F32)
        return carry

    lax.fori_loop(0, tiles, tile_step, 0)


def place_bits(sections, dest_ref, home_ref, *refs):
    shared, (weights_ref, out_ref, kept_ref, count_ref) = refs[:sections], refs[sections:]
    owners = out_ref.shape[0]
    batches, blocks = dest_ref.shape
    columns = weights_ref.shape[1]
    home = home_ref[0]
    own = pl.ds(pl.multiple_of(columns + home * batches * blocks, batches * blocks), batches * blocks)
    kept = shared[0][own, :].astype(F32)
    for ref in shared[1:]:
        kept = kept * ref[own, :].astype(F32)
    kept_ref[...] = kept
    for k, ref in enumerate(shared):
        weights_ref[home_ref[1 + k]] = ref[:columns, :]
    out_ref[...] = jnp.zeros_like(out_ref)

    def visit(micro, block, owner, slot):
        out_ref[owner, pl.ds(slot, 1), :] = kept_ref[pl.ds(micro * blocks + block, 1), :]

    walk_blocks(dest_ref, count_ref, owners, visit)


def join_blocks(slots, first_ref, weights_ref, table_ref, out_ref, keys_ref, found_ref, places_ref, sem):
    owners, columns = first_ref.shape[0], first_ref.shape[2]
    span = out_ref.shape[1]
    group = math.gcd(owners, 2)
    meta = first_ref[:, span : span + 2 * slots, :].astype(F32)
    keys_ref[...] = (meta[:, :slots] * 128.0 + meta[:, slots:]).astype(I32)
    copy = pltpu.make_async_copy(keys_ref, places_ref, sem)
    copy.start()
    weights = [weights_ref[j] for j in range(weights_ref.shape[0])]
    copy.wait()

    def step(turn, carry):
        base = turn * group
        values = first_ref[pl.ds(base, group), :span, :].reshape(group * span, columns)
        for source in range(group):
            for slot in range(slots):
                for row in range(span // slots):
                    place = places_ref[base + source, slot, row]
                    found_ref[pl.ds(source * span + slot * (span // slots) + row, 1), :] = table_ref[pl.ds(place, 1), :]
        for weight in weights:
            half = jnp.dot(values, weight, preferred_element_type=F32) * 0.5
            values = (values.astype(F32) + (half + half * jnp.tanh(half))).astype(BF16)
        joined = (values.astype(F32) * found_ref[...]).astype(BF16)
        out_ref[pl.ds(base, group)] = joined.reshape(group, span, columns)
        return carry

    lax.fori_loop(0, owners // group, step, 0)


def sum_groups(slots, first_ref, kept_ref, joined_ref, out_ref):
    owners, span, columns = joined_ref.shape
    groups = out_ref.shape[0]
    rows = span // slots
    step_size = math.gcd(owners, 8) if groups <= 128 else 1
    out_ref[...] = jnp.zeros_like(out_ref)
    sub = lax.broadcasted_iota(I32, (groups, rows), 0).astype(F32)

    def step(turn, carry):
        hot = []
        for source in range(step_size):
            at = turn * step_size + source
            meta = first_ref[at, span:, :].astype(F32)
            group = meta[2 * slots : 3 * slots] * 128.0 + meta[3 * slots : 4 * slots]
            group = jnp.where(kept_ref[at, :slots, :] > 0.5, group, -1.0)
            hot += [jnp.where(sub == group[j : j + 1], 1.0, 0.0).astype(BF16) for j in range(slots)]
        joined = joined_ref[pl.ds(turn * step_size, step_size)].reshape(step_size * span, columns)
        out_ref[...] += jnp.dot(jnp.concatenate(hot, axis=1), joined, preferred_element_type=F32)
        return carry

    lax.fori_loop(0, owners // step_size, step, 0)


def unpack_bits(bit_words):
    shifts = jnp.arange(16, dtype=jnp.int32)
    spread = jnp.right_shift(bit_words[..., None], shifts) & 1
    return spread.reshape(bit_words.shape[:-1] + (bit_words.shape[-1] * 16,))


def local(
    probe_values,
    probe_keys,
    group_ids,
    block_dest,
    filter_bits,
    section_weights,
    build_keys,
    build_values,
):
    sections = lax.axis_size("section")
    owners = lax.axis_size("owner")
    home = lax.axis_index("section").astype(I32)
    batches, block_count = block_dest.shape[:2]
    columns = probe_values.shape[2]
    rows = probe_values.shape[1] // block_count
    groups_all = GRP_DEV * sections * owners
    slots = batches * CAP
    span = slots * rows

    dest = block_dest.reshape(batches, block_count)
    blocks = probe_values.reshape(batches * block_count, rows, columns)
    counts = pltpu.SMEM((owners,), I32)
    first = run(
        functools.partial(pack_blocks, slots),
        "pack_blocks",
        [dest, blocks, probe_keys, group_ids],
        ((owners, span + FIELDS * slots, columns), BF16),
        [pltpu.VMEM((owners, FIELDS * slots, columns), F32), counts],
        scalars=1,
    )
    first = lax.all_to_all(first, "owner", split_axis=0, concat_axis=0, tiled=True)

    bits = unpack_bits(filter_bits[0]).astype(BF16).reshape(-1, rows)
    shared = jnp.concatenate([section_weights[0], bits], axis=0)
    paired = sections & (sections - 1) == 0

    def partner(index, k):
        return index ^ k if paired else (index - k) % sections

    received = [shared] + [
        lax.ppermute(shared, "section", [(partner(i, k), i) for i in range(sections)]) for k in range(1, sections)
    ]
    order = jnp.stack([home] + [lax.rem(partner(home, k) - home + sections, sections) for k in range(sections)])
    table = run(
        build_table,
        "build_table",
        [build_keys.reshape(-1, 128), build_values],
        ((KEYS_OWN, columns), F32),
        flops=2 * KEYS_OWN * build_keys.shape[0] * columns,
    )
    weights, kept = run(
        functools.partial(place_bits, sections),
        "place_bits",
        [dest, order] + received,
        [((sections, columns, columns), BF16), ((owners, 8, rows), F32)],
        [pltpu.VMEM((batches * block_count, rows), F32), counts],
        scalars=2,
    )
    kept, table = lax.optimization_barrier((kept, table))
    kept = lax.all_to_all(kept, "owner", split_axis=0, concat_axis=0, tiled=True)

    group = math.gcd(owners, 2)
    joined = run(
        functools.partial(join_blocks, slots),
        "join_blocks",
        [first, weights, table],
        ((owners, span, columns), BF16),
        [
            pltpu.VMEM((owners, slots, rows), I32),
            pltpu.VMEM((group * span, columns), F32),
            pltpu.SMEM((owners, slots, rows), I32),
            pltpu.SemaphoreType.DMA,
        ],
        flops=2 * KEYS_OWN * owners * span * columns,
    )
    sums = run(
        functools.partial(sum_groups, slots),
        "sum_groups",
        [first, kept, joined],
        ((groups_all, columns), F32),
        flops=2 * groups_all * owners * span * columns,
    )
    parts = sums.reshape(sections * owners, GRP_DEV, columns)
    parts = lax.all_to_all(parts, ("section", "owner"), split_axis=0, concat_axis=0, tiled=True)
    return jnp.sum(parts, axis=0)


def solution(mesh):
    placed = (
        P("section", "owner", None),
        P("section", "owner"),
        P("section", "owner"),
        P("section", "owner", None),
        P("section", None, "owner"),
        P("section", None, None),
        P("owner"),
        P("owner", None),
    )
    return jax.shard_map(
        local, mesh=mesh, in_specs=placed, out_specs=P(("section", "owner"), None), check_vma=False
    )
```

time: 224 us -> 63.5 us (0.28)
  waiting for transfers between devices: 125 us -> 14.5 us
  other arithmetic: 25.6 us -> 0.64 us
  Pallas kernels: 0 us -> 17.7 us
  local copies, waits for them, and re-layouts: 20.3 us -> 3.55 us
  between operations: 13.6 us -> 0.14 us
  matrix products: 5.02 us -> 0 us
  blocking collectives: 16.6 us -> 13.2 us
    unnamed x2 -> x0, waiting for transfers between devices: 117 us -> none
    scatter-add x1 -> x0, other arithmetic: 22.8 us -> none  [local(): jax.ops.segment_sum(build_values.astype(jnp.float32), build_keys, num_seg...]
    pallas_call x0 -> x5, Pallas kernels: none -> 17.7 us  [run(): pl.pallas_call(kernel, out_shape=shapes if several else shapes[0], in_spe...]
    all_gather x2 -> x0, blocking collectives: 16.6 us -> none  [the longest x1 8.67 us: local(): lax.all_gather(section_weights, 'section', axis=0, tiled=True)]
    all_to_all x0 -> x1, blocking collectives: none -> 13.2 us  [local(): lax.all_to_all(parts, ('section', 'owner'), split_axis=0, concat_axis=0,...]
    gather x7 -> x0, local copies, waits for them, and re-layouts: 13.2 us -> none  [the longest x2 10.9 us: add_block(): matched = jnp.take(key_table, part_keys, axis=0)]
    all_to_all x3 -> x2, waiting for transfers between devices: 8.01 us -> 14.5 us  [the longest x1 14.5 us: local(): lax.all_to_all(first, 'owner', split_axis=0, concat_axis=0, tiled=True)]
    all_to_all x3 -> x2, starting transfers between devices: 15 us -> 9.82 us  [the longest x1 6.5 us: local(): lax.all_to_all(first, 'owner', split_axis=0, concat_axis=0, tiled=True)]
  transfers between devices with their start and end apart: 4 -> 5, of which waited for: 3 -> 1; matrix products, arithmetic and copies ran while one was open for 14% -> 1% of each run, Pallas kernels for 0% -> 24%
where the time goes in v2:
time: 63.5 us; the launch traced here: 63.1 us
  Pallas kernels  17.7 us (28%)
  waiting for transfers between devices  14.5 us (23%)
  starting transfers between devices  13.4 us (21%)
  blocking collectives  13.2 us (21%)
  local copies, waits for them, and re-layouts  3.55 us (6%)
  other arithmetic  0.64 us (1%)
    pallas_call x5, Pallas kernels, run(): pl.pallas_call(kernel, out_shape=shapes if several else shapes[0], in_spe...  17.7 us
    all_to_all x1, waiting for transfers between devices, local(): lax.all_to_all(first, 'owner', split_axis=0, concat_axis=0, tiled=True)  14.5 us
    all_to_all x1, blocking collectives, local(): lax.all_to_all(parts, ('section', 'owner'), split_axis=0, concat_axis=0,...  13.2 us
    all_to_all x1, starting transfers between devices, local(): lax.all_to_all(first, 'owner', split_axis=0, concat_axis=0, tiled=True)  6.5 us
    ppermute x3, starting transfers between devices, local(): lax.ppermute(shared, 'section', [(partner(i, k), i) for i in range(sectio...  3.55 us
    all_to_all x1, starting transfers between devices, local(): lax.all_to_all(kept, 'owner', split_axis=0, concat_axis=0, tiled=True)  3.33 us
    unnamed x18, local copies, waits for them, and re-layouts  3.13 us
  transfers between devices with their start and end apart: 5, of which 1 were waited for; matrix products, arithmetic and copies ran while one was open for 1% of the time, Pallas kernels for 24%

profile of v2, /device:TPU:0, one launch (start us, length us, event | category | flops | bytes accessed | tf_op | source)
XLA Modules:
  0.0 63.1 jit_solution(12381692020714145441)
XLA Ops:
  0.0 1.0 %copy-done = bf16[2,1024,128]{2,1,0:T(8,128)(2,1)S(1)} copy-done((bf16[2,1024,128]{2,1,0:T(8,128)(2,1)S(1)}, bf16[2,1024,128]{2,1,0:T(8,128)(2,1)}, u32[]{:S(2)}) %copy-start) | copy-done | bytes 524312
  1.0 0.7 %copy-done.1 = s32[2,1024]{1,0:T(2,128)S(1)} copy-done((s32[2,1024]{1,0:T(2,128)S(1)}, s32[2,1024]{1,0:T(2,128)}, u32[]{:S(2)}) %copy-start.1) | copy-done | bytes 8216
  1.7 0.7 %copy-done.2 = s32[2,1024]{1,0:T(2,128)S(1)} copy-done((s32[2,1024]{1,0:T(2,128)S(1)}, s32[2,1024]{1,0:T(2,128)}, u32[]{:S(2)}) %copy-start.2) | copy-done | bytes 8216
  2.4 0.7 %copy-done.3 = s32[2,8,1]{1,2,0:T(1,128)S(1)} copy-done((s32[2,8,1]{1,2,0:T(1,128)S(1)}, s32[2,8,1]{1,2,0:T(1,128)}, u32[]{:S(2)}) %copy-start.3) | copy-done | bytes 88
  3.1 1.8 %pack_blocks.1 = bf16[8,528,128]{2,1,0:T(8,128)(2,1)} custom-call(s32[2,8]{1,0:T(2,128)S(1)} %bitcast.18, bf16[16,128,128]{2,1,0:T(8,128)(2,1)S(1)} %bitcast.16, s32[2,1024]{1,0:T(2,128)S(1)} %copy-done.1, s32[2,1024]{1,0:T(2,128)S(1)} %copy-done.2), custom_call_target="tpu_custom_call" | custom-call | tf_op jit(solution)/shard_map/pack_blocks/pallas_call | solution.py:28
  4.9 6.5 %all-to-all-start = ((bf16[8,528,128]{2,1,0:T(8,128)(2,1)}), bf16[8,528,128]{2,1,0:T(8,128)(2,1)S(1)}, u32[]{:S(2)}, u32[]{:S(2)}) async-start(bf16[8,528,128]{2,1,0:T(8,128)(2,1)} %pack_blocks.1), calls=%async_computation | async-start | bytes 2162688 | tf_op jit(solution)/shard_map/all_to_all | solution.py:211
  11.5 0.1 shift_right_arithmetic.26
  11.6 0.1 shift_right_arithmetic.27
  11.7 0.1 shift_right_arithmetic.29
  11.8 1.6 %collective-permute-start = (bf16[192,128]{1,0:T(8,128)(2,1)S(1)}, bf16[192,128]{1,0:T(8,128)(2,1)S(1)}, u32[]{:S(2)}, u32[]{:S(2)}) collective-permute-start(bf16[192,128]{1,0:T(8,128)(2,1)S(1)} %pad_maximum_fusion.refs_0_), channel_id=1, source_target_pairs={{8,0},{0,8},{24,16},{16,24},{9,1},{1,9},{25,17},{17,25},{10,2},{2,... | collective-permute-start | bytes 147464 | tf_op jit(solution)/shard_map/ppermute | solution.py:221
  13.4 1.5 %collective-permute-start.1 = (bf16[192,128]{1,0:T(8,128)(2,1)S(1)}, bf16[192,128]{1,0:T(8,128)(2,1)S(1)}, u32[]{:S(2)}, u32[]{:S(2)}) collective-permute-start(bf16[192,128]{1,0:T(8,128)(2,1)S(1)} %pad_maximum_fusion.refs_0_), channel_id=1, source_target_pairs={{16,0},{24,8},{0,16},{8,24},{17,1},{25,9},{1,17},{9,25},{18,2},{26... | collective-permute-start | bytes 147464 | tf_op jit(solution)/shard_map/ppermute | solution.py:221
  14.9 0.5 collective-permute-start.2
  15.4 7.4 %build_table.1.table_ref = f32[2048,128]{1,0:T(8,128)S(1)} custom-call(s32[32,128]{1,0:T(8,128)S(1)} %bitcast.20, bf16[4096,128]{1,0:T(8,128)(2,1)S(1)} %copy-done.5), custom_call_target="tpu_custom_call" | custom-call | flops 2147483648 | bytes 2113536 | tf_op jit(solution)/shard_map/build_table/pallas_call | solution.py:28
  22.8 0.1 stack.19.home_ref
  22.9 0.0 collective-permute-done.refs_1_
  22.9 0.0 collective-permute-done.1.refs_2_
  22.9 1.3 %place_bits.1 = (bf16[4,128,128]{2,1,0:T(8,128)(2,1)S(1)}, f32[8,8,128]{2,1,0:T(8,128)}) custom-call(s32[2,8]{1,0:T(2,128)S(1)} %bitcast.19, s32[5]{0:T(128)S(1)} %stack.19.home_ref, bf16[192,128]{1,0:T(8,128)(2,1)S(1)} %pad_maximum_fusion.refs_0_, bf16[192,128]{1,0:T(8,128)(2,1)S(1)} %collective-permute-done.refs_1_, ...), custom_call_target="tpu_custom_call" | custom-call | tf_op jit(solution)/shard_map/place_bits/pallas_call | solution.py:28
  24.2 14.5 %all-to-all-done.first_ref = bf16[8,528,128]{2,1,0:T(8,128)(2,1)S(1)} async-done(((bf16[8,528,128]{2,1,0:T(8,128)(2,1)}), bf16[8,528,128]{2,1,0:T(8,128)(2,1)S(1)}, u32[]{:S(2)}, u32[]{:S(2)}) %all-to-all-start) | async-done | bytes 1081376 | tf_op jit(solution)/shard_map/all_to_all | solution.py:211
  38.7 3.3 %all-to-all-start.1 = ((f32[8,8,128]{2,1,0:T(8,128)}), f32[8,8,128]{2,1,0:T(8,128)S(1)}, u32[]{:S(2)}, u32[]{:S(2)}) async-start(f32[8,8,128]{2,1,0:T(8,128)} %get-tuple-element.10), calls=%async_computation.1 | async-start | bytes 65536 | tf_op jit(solution)/shard_map/all_to_all | solution.py:240
  42.0 6.8 %join_blocks.1.joined_ref = bf16[8,512,128]{2,1,0:T(8,128)(2,1)S(1)} custom-call(bf16[8,528,128]{2,1,0:T(8,128)(2,1)S(1)} %all-to-all-done.first_ref, bf16[4,128,128]{2,1,0:T(8,128)(2,1)S(1)} %get-tuple-element.11.weights_ref, f32[2048,128]{1,0:T(8,128)S(1)} %build_table.1.table_ref), custom_call_target="tpu_custom_call" | custom-call | flops 2147483648 | bytes 4423688 | tf_op jit(solution)/shard_map/join_blocks/pallas_call | solution.py:28
  48.8 0.0 all-to-all-done.1.kept_ref
  48.8 0.4 sum_groups.1
  49.3 13.2 %all_to_all.15 = f32[32,4,128]{2,1,0:T(4,128)S(1)} all-to-all(f32[32,4,128]{2,1,0:T(4,128)S(1)} %bitcast.17), channel_id=1, replica_groups=mesh['section'=4,'owner'=8] {'section','owner'}, dimensions={0} | all-to-all | bytes 131072 | tf_op jit(solution)/shard_map/all_to_all | solution.py:264
  62.5 0.6 reduce_sum.9
  (18 shorter events, 0.0 us)
Async XLA Ops:
  0.0 1.0 %copy-start = (bf16[2,1024,128]{2,1,0:T(8,128)(2,1)S(1)}, bf16[2,1024,128]{2,1,0:T(8,128)(2,1)}, u32[]{:S(2)}) copy-start(bf16[2,1024,128]{2,1,0:T(8,128)(2,1)} %param.8) | copy-start | bytes 1572868
  1.0 0.7 %copy-start.1 = (s32[2,1024]{1,0:T(2,128)S(1)}, s32[2,1024]{1,0:T(2,128)}, u32[]{:S(2)}) copy-start(s32[2,1024]{1,0:T(2,128)} %keys_ref.1) | copy-start | bytes 24580
  1.7 0.7 %copy-start.2 = (s32[2,1024]{1,0:T(2,128)S(1)}, s32[2,1024]{1,0:T(2,128)}, u32[]{:S(2)}) copy-start(s32[2,1024]{1,0:T(2,128)} %groups_ref.1) | copy-start | bytes 24580
  2.4 0.7 %copy-start.3 = (s32[2,8,1]{1,2,0:T(1,128)S(1)}, s32[2,8,1]{1,2,0:T(1,128)}, u32[]{:S(2)}) copy-start(s32[2,8,1]{1,2,0:T(1,128)} %param.11) | copy-start | bytes 196
  4.9 6.5 %copy-start.8 = (s32[1,8,64]{2,1,0:T(8,128)S(1)}, s32[1,8,64]{2,1,0:T(8,128)}, u32[]{:S(2)}) copy-start(s32[1,8,64]{2,1,0:T(8,128)} %param.12) | copy-start | bytes 6148
  4.9 6.9 %copy-start.7 = (bf16[1,128,128]{2,1,0:T(8,128)(2,1)S(1)}, bf16[1,128,128]{2,1,0:T(8,128)(2,1)}, u32[]{:S(2)}) copy-start(bf16[1,128,128]{2,1,0:T(8,128)(2,1)} %param.13) | copy-start | bytes 98308
  4.9 10.5 %copy-start.5 = (bf16[4096,128]{1,0:T(8,128)(2,1)S(1)}, bf16[4096,128]{1,0:T(8,128)(2,1)}, u32[]{:S(2)}) copy-start(bf16[4096,128]{1,0:T(8,128)(2,1)} %values_ref.1) | copy-start | bytes 3145732
  4.9 10.5 %copy-start.6 = (s32[4096]{0:T(1024)S(1)}, s32[4096]{0:T(1024)}, u32[]{:S(2)}) copy-start(s32[4096]{0:T(1024)} %param.14) | copy-start | bytes 49156
  4.9 33.8 %all-to-all-start = ((bf16[8,528,128]{2,1,0:T(8,128)(2,1)}), bf16[8,528,128]{2,1,0:T(8,128)(2,1)S(1)}, u32[]{:S(2)}, u32[]{:S(2)}) async-start(bf16[8,528,128]{2,1,0:T(8,128)(2,1)} %pack_blocks.1), calls=%async_computation | async-start | bytes 2162688 | tf_op jit(solution)/shard_map/all_to_all | solution.py:211
  11.8 11.0 %collective-permute-start = (bf16[192,128]{1,0:T(8,128)(2,1)S(1)}, bf16[192,128]{1,0:T(8,128)(2,1)S(1)}, u32[]{:S(2)}, u32[]{:S(2)}) collective-permute-start(bf16[192,128]{1,0:T(8,128)(2,1)S(1)} %pad_maximum_fusion.refs_0_), channel_id=1, source_target_pairs={{8,0},{0,8},{24,16},{16,24},{9,1},{1,9},{25,17},{17,25},{10,2},{2,... | collective-permute-start | bytes 147464 | tf_op jit(solution)/shard_map/ppermute | solution.py:221
  13.4 9.5 %collective-permute-start.1 = (bf16[192,128]{1,0:T(8,128)(2,1)S(1)}, bf16[192,128]{1,0:T(8,128)(2,1)S(1)}, u32[]{:S(2)}, u32[]{:S(2)}) collective-permute-start(bf16[192,128]{1,0:T(8,128)(2,1)S(1)} %pad_maximum_fusion.refs_0_), channel_id=1, source_target_pairs={{16,0},{24,8},{0,16},{8,24},{17,1},{25,9},{1,17},{9,25},{18,2},{26... | collective-permute-start | bytes 147464 | tf_op jit(solution)/shard_map/ppermute | solution.py:221
  14.9 8.0 %collective-permute-start.2 = (bf16[192,128]{1,0:T(8,128)(2,1)S(1)}, bf16[192,128]{1,0:T(8,128)(2,1)S(1)}, u32[]{:S(2)}, u32[]{:S(2)}) collective-permute-start(bf16[192,128]{1,0:T(8,128)(2,1)S(1)} %pad_maximum_fusion.refs_0_), channel_id=1, source_target_pairs={{24,0},{16,8},{8,16},{0,24},{25,1},{17,9},{9,17},{1,25},{26,2},{18... | collective-permute-start | bytes 147464 | tf_op jit(solution)/shard_map/ppermute | solution.py:221
  15.4 7.5 %copy-start.4 = (s32[2,8,1]{1,2,0:T(1,128)S(1)}, s32[2,8,1]{1,2,0:T(1,128)}, u32[]{:S(2)}) copy-start(s32[2,8,1]{1,2,0:T(1,128)} %param.11) | copy-start | bytes 196
  38.7 10.1 %all-to-all-start.1 = ((f32[8,8,128]{2,1,0:T(8,128)}), f32[8,8,128]{2,1,0:T(8,128)S(1)}, u32[]{:S(2)}, u32[]{:S(2)}) async-start(f32[8,8,128]{2,1,0:T(8,128)} %get-tuple-element.10), calls=%async_computation.1 | async-start | bytes 65536 | tf_op jit(solution)/shard_map/all_to_all | solution.py:240
